TPU v7x, 512 devices: a whole 4x8x8 slice. The times are simulated.
512 devices in a mesh: sub: 128 (over z, y, core), grp: 4 (over x).
Axes of the slice: x: 4, y: 8, z: 8, core: 2. Of those that a mesh axis runs over, the one named last changes fastest.
Arguments:
- schur: bfloat16 [128, 2048, 2048], P('sub', 'grp'), may hold values from -0.125 to 0.125
- rhs: float32 [128, 2048, 192], P('sub', 'grp'), may hold values from -6 to 6
- start: float32 [128, 2048, 192], P('sub', 'grp'), may hold values from -6 to 6
- project: bfloat16 [128, 32, 4096], P('sub', 'grp'), may hold values from -0.75 to 0.75
- coarse_basis: bfloat16 [128, 8, 2048], P('sub', None, 'grp'), may hold values from -0.375 to 0.375
- owner_of_face: int32 [128, 32, 1], replicated, may hold values from 0 to 4; in each aligned block of 32 rows (0 to 31, 32 to 63, ..., all dimensions but the last counted through in order) at most 8 rows name the same one
- mortar_of_face: int32 [128, 32], replicated, may hold values from 0 to 15
- mortar_order: int32 [128, 16], replicated, may hold values from 3 to 7
- subdomain_map: int32 [128], replicated, may hold values from 0 to 127, each once
- vertex_ids: int32 [128, 8], replicated, may hold values from 0 to 255, all different within a row
Outputs:
- solution: float32 [128, 2048, 192], P('sub', 'grp')
Inputs may be any that keep to these rules, and one draw needn't show every extreme that they name: `owner_of_face`: the 32 faces of one subdomain name one offset at most 8 times. `mortar_of_face`: faces with the same owner and the same number lie on one mortar. `mortar_order`: row o holds the orders of the mortars owned by index o. `subdomain_map`: each subdomain once. `vertex_ids`: the 8 vertices of a subdomain differ; every vertex belongs to some subdomain.
All inputs are finite; a program needn't handle non-finite values.
Results may differ from a plain program's by a relative error of at most 0.0031.
Values may be sent and summed in bfloat16 or wider, within the bound.
A program may use at most 64 MiB of HBM per device.

v0:
```python
import jax
import jax.numpy as jnp
from jax import lax
from jax.sharding import Mesh
from jax.sharding import PartitionSpec as P

DEG = 8
FPTS = 64
MODES = 64
MORT_OWN = 16
ITERS = 2
REACH = 2
CAP = 8
SUB = ("sub_0", "sub_1", "sub_2")
relax_weight = 0.5
coarse_weight = 0.5


def joined_along(parts, dim):
    parts = jnp.moveaxis(parts, 0, dim)
    lengths = parts.shape
    return parts.reshape(*lengths[:dim], lengths[dim] * lengths[dim + 1], *lengths[dim + 2 :])


def sent_to_all(value, axis):
    copies = jnp.broadcast_to(value, (lax.axis_size(axis), *value.shape))
    return lax.all_to_all(copies, axis, split_axis=0, concat_axis=0, tiled=True)


def gathered_copies(value, axis, dim):
    return joined_along(sent_to_all(value, axis), dim)


def passed_along(value, axis, steps):
    count = lax.axis_size(axis)
    pairs = [(source, (source + steps) % count) for source in range(count)]
    return lax.ppermute(value, axis, pairs)


def taken_together(value, axis):
    return sent_to_all(value, axis).sum(axis=0)


def filled_up(lines, length):
    spare = -len(lines) % length
    return jnp.pad(lines, [(0, spare)] + [(0, 0)] * (lines.ndim - 1))


def whole_of(value, axes, dim):
    far, near = axes
    parts = sent_to_all(sent_to_all(value, far), near)
    return joined_along(parts.swapaxes(0, 1).reshape(-1, *value.shape), dim)


def split_up(value, dim, length):
    before, after = (value.shape[:dim], value.shape[dim + 1 :])
    return jnp.moveaxis(value.reshape(*before, length, -1, *after), dim, 0)


def sent_and_summed(value, axis, dim):
    parts = split_up(value, dim, lax.axis_size(axis))
    arrived = lax.all_to_all(parts, axis, split_axis=0, concat_axis=0, tiled=True)
    return arrived.sum(axis=0)


def summed_rows(value, axes, dim):
    far, near = axes
    parts = split_up(value, dim, lax.axis_size(far))
    nearer = sent_and_summed(parts, near, dim + 1)
    arrived = lax.all_to_all(nearer, far, split_axis=0, concat_axis=0, tiled=True)
    return arrived.sum(axis=0)


def sum_by_parts(value, axes):
    lines = value.reshape(-1, value.shape[-1])
    padded = filled_up(lines, lax.axis_size(axes[0]) * lax.axis_size(axes[1]))
    whole = whole_of(summed_rows(padded, axes, 0), axes, 0)
    return lax.slice_in_dim(whole, 0, len(lines)).reshape(value.shape)


def body(
    schur,
    rhs,
    start,
    project,
    coarse_basis,
    owner_of_face,
    mortar_of_face,
    mortar_order,
    subdomain_map,
    vertex_ids,
):
    highest = lax.Precision.HIGHEST
    contract_first = (((0,), (0,)), ((), ()))
    sub_count = lax.axis_size(SUB)
    position = lax.axis_index(SUB)
    all_faces = owner_of_face.shape[1]
    own_faces = project.shape[1]
    own_rows = schur.shape[1]
    neighbours = 2 * REACH + 1
    capacity = CAP
    vertices = 2 * sub_count
    held = jnp.take(owner_of_face[:, :, 0], subdomain_map, axis=0)
    mortar_local = jnp.take(mortar_of_face, subdomain_map, axis=0)
    face_index = jnp.arange(all_faces, dtype=jnp.int32)
    earlier = face_index[None, :] < face_index[:, None]
    ranks = jnp.sum(
        ((held[:, :, None] == held[:, None, :]) & earlier[None, :, :]).astype(jnp.int32), axis=2
    )
    my_held = lax.dynamic_index_in_dim(held, position, 0, keepdims=False)
    my_ranks = lax.dynamic_index_in_dim(ranks, position, 0, keepdims=False)
    slot_ids = my_held * capacity + my_ranks
    send_table = (
        jnp.arange(neighbours * capacity, dtype=jnp.int32)[:, None] == slot_ids[None, :]
    ).astype(jnp.bfloat16)
    links = jnp.arange(neighbours, dtype=jnp.int32)
    senders = jnp.mod(position - links + REACH, sub_count)
    from_held = jnp.take(held, senders, axis=0)
    from_mortar = jnp.take(mortar_local, senders, axis=0)
    from_ranks = jnp.take(ranks, senders, axis=0)
    incoming = (from_held == links[:, None]).astype(jnp.float32)
    mortar_hot = (
        from_mortar[:, :, None] == jnp.arange(MORT_OWN, dtype=jnp.int32)[None, None, :]
    ).astype(jnp.float32)
    rank_hot = (
        from_ranks[:, :, None] == jnp.arange(capacity, dtype=jnp.int32)[None, None, :]
    ).astype(jnp.float32)
    counts = jnp.einsum("jfk,jf->k", mortar_hot, incoming)
    degree = jnp.arange(MODES, dtype=jnp.int32)
    orders = lax.dynamic_index_in_dim(mortar_order, position, 0, keepdims=False)[:, None]
    keep_mask = ((degree[None, :] // DEG <= orders) & (degree[None, :] % DEG <= orders)).astype(
        jnp.float32
    )
    divisor = jnp.maximum(counts, 1.0)
    joined = jnp.einsum("jfk,jfc->kjc", mortar_hot * incoming[:, :, None], rank_hot)
    owner_table = joined.reshape(MORT_OWN, neighbours * capacity).astype(jnp.bfloat16)
    my_corners = lax.dynamic_index_in_dim(
        jnp.take(vertex_ids, subdomain_map, axis=0), position, 0, keepdims=False
    )
    corner_hot = (my_corners[:, None] == jnp.arange(vertices, dtype=jnp.int32)[None, :]).astype(
        jnp.float32
    )
    coarse_wide = coarse_basis[0].astype(jnp.float32)
    tables = project[0].reshape(own_faces, MODES, FPTS)
    matrix = schur[0]
    target = rhs[0]
    traces = start[0]
    for repeat in range(ITERS):
        trace_b = traces.astype(jnp.bfloat16)
        product = jnp.dot(
            matrix, gathered_copies(trace_b, "grp", 0), preferred_element_type=jnp.float32
        )
        residual = (product - target).astype(jnp.bfloat16)
        face_res = residual.reshape(own_faces, FPTS, -1)
        coeffs = jnp.einsum(
            "fmp,fpr->fmr", tables, face_res, preferred_element_type=jnp.float32
        ).astype(jnp.bfloat16)
        grouped = lax.all_to_all(coeffs, "grp", split_axis=2, concat_axis=0, tiled=True)
        part_rhs = grouped.shape[2]
        payload = grouped.reshape(all_faces, MODES * part_rhs)
        outgoing = jnp.dot(send_table, payload, preferred_element_type=jnp.float32).astype(
            jnp.bfloat16
        )
        blocks = outgoing.reshape(neighbours, capacity, -1)
        arrivals = []
        for link in range(neighbours):
            arrivals.append(passed_along(blocks[link], SUB, link - REACH))
        arrived = jnp.concatenate(arrivals, axis=0)
        mortar_sums = jnp.dot(owner_table, arrived, preferred_element_type=jnp.float32)
        shaped = mortar_sums.reshape(MORT_OWN, MODES, part_rhs) / divisor[:, None, None]
        shaped = shaped * keep_mask[:, :, None]
        averages = shaped.reshape(MORT_OWN, MODES * part_rhs).astype(jnp.bfloat16)
        replies = lax.dot_general(
            owner_table, averages, contract_first, preferred_element_type=jnp.float32
        ).astype(jnp.bfloat16)
        reply_blocks = replies.reshape(neighbours, capacity, -1)
        answers = []
        for link in range(neighbours):
            answers.append(passed_along(reply_blocks[link], SUB, REACH - link))
        answered = jnp.concatenate(answers, axis=0)
        own_back = lax.dot_general(
            send_table, answered, contract_first, preferred_element_type=jnp.float32
        ).astype(jnp.bfloat16)
        returned = lax.all_to_all(
            own_back.reshape(all_faces, MODES, part_rhs),
            "grp",
            split_axis=0,
            concat_axis=2,
            tiled=True,
        )
        lifted = jnp.einsum(
            "fmp,fmr->fpr", tables, returned, preferred_element_type=jnp.float32
        ).reshape(own_rows, -1)
        partial_value = jnp.dot(coarse_wide, lifted, precision=highest)
        summed = taken_together(partial_value, "grp")
        spread = lax.dot_general(corner_hot, summed, contract_first, precision=highest)
        vertex = sum_by_parts(spread, (("sub_0", "sub_1"), "sub_2"))
        picked = jnp.dot(corner_hot, vertex, precision=highest)
        coarse_corr = lax.dot_general(coarse_wide, picked, contract_first, precision=highest)
        traces = traces - relax_weight * lifted - coarse_weight * coarse_corr
    return traces[None]


def solution(mesh):
    finer = Mesh(
        mesh.devices.reshape(8, 8, 2, mesh.shape["grp"]), ("sub_0", "sub_1", "sub_2", "grp")
    )
    placed = (
        P(SUB, "grp", None),
        P(SUB, "grp", None),
        P(SUB, "grp", None),
        P(SUB, "grp", None),
        P(SUB, None, "grp"),
        P(),
        P(),
        P(),
        P(),
        P(),
    )
    return jax.shard_map(
        body, mesh=finer, in_specs=placed, out_specs=P(SUB, "grp", None), check_vma=False
    )
```

profile of v0, /device:TPU:1, one launch (start us, length us, event | category | flops | bytes accessed | tf_op | source)
XLA Modules:
  0.0 286.5 jit_solution(6291105881597627095)
XLA Ops:
  0.0 1.2 bitcast_convert_fusion
  2.2 5.0 %all-to-all-start = ((bf16[4,512,192]{1,2,0:T(8,128)(2,1)}), bf16[4,512,192]{1,2,0:T(8,128)(2,1)S(1)}, u32[]{:S(2)}, u32[]{:S(2)}) async-start(bf16[4,512,192]{1,2,0:T(8,128)(2,1)} %broadcast_in_dim.48), calls=%async_computation | async-start | bytes 1572864 | tf_op jit(solution)/shard_map/all_to_all | solution.py:27
  9.8 1.4 broadcast_select_fusion
  11.8 1.3 fusion.68
  13.3 1.4 gather_fusion.4
  15.4 1.0 reshape_squeeze.3
  20.9 1.0 reshape.341
  21.9 4.2 %all-to-all-start.1 = ((bf16[4,2,12288]{2,1,0:T(2,128)(2,1)}), bf16[4,2,12288]{2,1,0:T(2,128)(2,1)S(1)}, u32[]{:S(2)}, u32[]{:S(2)}) async-start(bf16[4,2,12288]{2,1,0:T(2,128)(2,1)} %reshape.341), calls=%async_computation.1 | async-start | bytes 393216 | tf_op jit(solution)/shard_map/all_to_all | solution.py:158
  26.2 5.1 %all-to-all-done.1 = bf16[4,2,12288]{2,1,0:T(2,128)(2,1)S(1)} async-done(((bf16[4,2,12288]{2,1,0:T(2,128)(2,1)}), bf16[4,2,12288]{2,1,0:T(2,128)(2,1)S(1)}, u32[]{:S(2)}, u32[]{:S(2)}) %all-to-all-start.1) | async-done | bytes 196640 | tf_op jit(solution)/shard_map/all_to_all | solution.py:158
  33.0 13.6 %collective-permute-start = (bf16[8,3072]{1,0:T(8,128)(2,1)S(1)}, bf16[8,3072]{1,0:T(8,128)(2,1)S(1)}, u32[]{:S(2)}, u32[]{:S(2)}) collective-permute-start(bf16[8,3072]{1,0:T(8,128)(2,1)S(1)} %get-tuple-element.28), channel_id=1, source_target_pairs={{0,504},{4,508},{8,0},{12,4},{16,8},{20,12},{24,16},{28,20},{32,24... | collective-permute-start | bytes 147464 | tf_op jit(solution)/shard_map/ppermute | solution.py:37
  46.7 1.9 collective-permute-start.4
  48.6 1.9 collective-permute-start.3
  50.6 4.9 %collective-permute-start.1 = (bf16[8,3072]{1,0:T(8,128)(2,1)S(1)}, bf16[8,3072]{1,0:T(8,128)(2,1)S(1)}, u32[]{:S(2)}, u32[]{:S(2)}) collective-permute-start(bf16[8,3072]{1,0:T(8,128)(2,1)S(1)} %get-tuple-element.27), channel_id=1, source_target_pairs={{0,508},{4,0},{8,4},{12,8},{16,12},{20,16},{24,20},{28,24},{32,28}... | collective-permute-start | bytes 147464 | tf_op jit(solution)/shard_map/ppermute | solution.py:37
  58.5 1.9 collective-permute-start.5
  60.4 12.5 %collective-permute-start.9 = (bf16[8,3072]{1,0:T(8,128)(2,1)S(1)}, bf16[8,3072]{1,0:T(8,128)(2,1)S(1)}, u32[]{:S(2)}, u32[]{:S(2)}) collective-permute-start(bf16[8,3072]{1,0:T(8,128)(2,1)S(1)} %get-tuple-element.19), channel_id=1, source_target_pairs={{0,504},{4,508},{8,0},{12,4},{16,8},{20,12},{24,16},{28,20},{32,24... | collective-permute-start | bytes 147464 | tf_op jit(solution)/shard_map/ppermute | solution.py:37
  72.9 2.5 collective-permute-start.8
  75.5 3.0 %collective-permute-start.6 = (bf16[8,3072]{1,0:T(8,128)(2,1)S(1)}, bf16[8,3072]{1,0:T(8,128)(2,1)S(1)}, u32[]{:S(2)}, u32[]{:S(2)}) collective-permute-start(bf16[8,3072]{1,0:T(8,128)(2,1)S(1)} %get-tuple-element.22), channel_id=1, source_target_pairs={{0,4},{4,8},{8,12},{12,16},{16,20},{20,24},{24,28},{28,32},{32,36}... | collective-permute-start | bytes 147464 | tf_op jit(solution)/shard_map/ppermute | solution.py:37
  78.5 1.1 collective-permute-done.6
  81.8 3.4 %all-to-all-start.2 = ((bf16[4,2,12288]{2,1,0:T(2,128)(2,1)}), bf16[4,2,12288]{2,1,0:T(2,128)(2,1)S(1)}, u32[]{:S(2)}, u32[]{:S(2)}) async-start(bf16[4,2,12288]{2,1,0:T(2,128)(2,1)} %reshape.343), calls=%async_computation.2 | async-start | bytes 393216 | tf_op jit(solution)/shard_map/all_to_all | solution.py:184
  86.7 3.6 %all-to-all-done.2 = bf16[4,2,12288]{2,1,0:T(2,128)(2,1)S(1)} async-done(((bf16[4,2,12288]{2,1,0:T(2,128)(2,1)}), bf16[4,2,12288]{2,1,0:T(2,128)(2,1)S(1)}, u32[]{:S(2)}, u32[]{:S(2)}) %all-to-all-start.2) | async-done | bytes 196640 | tf_op jit(solution)/shard_map/all_to_all | solution.py:184
  92.0 3.3 %all-to-all-start.3 = ((f32[4,8,192]{2,1,0:T(8,128)}), f32[4,8,192]{2,1,0:T(8,128)S(1)}, u32[]{:S(2)}, u32[]{:S(2)}) async-start(f32[4,8,192]{2,1,0:T(8,128)} %broadcast_in_dim.83), calls=%async_computation.3 | async-start | bytes 65536 | tf_op jit(solution)/shard_map/all_to_all | solution.py:27
  95.9 3.6 %all-to-all-done.3 = f32[4,8,192]{2,1,0:T(8,128)S(1)} async-done(((f32[4,8,192]{2,1,0:T(8,128)}), f32[4,8,192]{2,1,0:T(8,128)S(1)}, u32[]{:S(2)}, u32[]{:S(2)}) %all-to-all-start.3) | async-done | bytes 24608 | tf_op jit(solution)/shard_map/all_to_all | solution.py:27
  99.9 11.6 %all_to_all.126 = f32[2,64,2,192]{3,1,2,0:T(8,128)S(1)} all-to-all(f32[2,64,2,192]{3,1,2,0:T(8,128)S(1)} %convolution_bitcast_fusion.1), channel_id=1, replica_groups=mesh['sub_0'=8,'sub_1'=8,'sub_2'=2,'grp'=4] {'sub_2'}, dimensions={0} | all-to-all | bytes 393216 | tf_op jit(solution)/shard_map/all_to_all | solution.py:62
  111.7 15.4 %all_to_all.127 = f32[64,2,192]{2,1,0:T(2,128)S(1)} all-to-all(f32[64,2,192]{2,1,0:T(2,128)S(1)} %copy.170), channel_id=1, replica_groups=mesh['sub_0'=8,'sub_1'=8,'sub_2'=2,'grp'=4] {'sub_0','sub_1'}, dimensions={0} | all-to-all | bytes 196608 | tf_op jit(solution)/shard_map/all_to_all | solution.py:70
  127.9 5.5 %all-to-all-start.6 = ((f32[64,2,192]{2,1,0:T(2,128)}), f32[64,2,192]{2,1,0:T(2,128)}, u32[]{:S(2)}, u32[]{:S(2)}) async-start(f32[64,2,192]{2,1,0:T(2,128)} %broadcast_in_dim.84), calls=%async_computation.6 | async-start | bytes 262144 | tf_op jit(solution)/shard_map/all_to_all | solution.py:27
  133.6 11.2 %all-to-all-done.6 = f32[64,2,192]{2,1,0:T(2,128)} async-done(((f32[64,2,192]{2,1,0:T(2,128)}), f32[64,2,192]{2,1,0:T(2,128)}, u32[]{:S(2)}, u32[]{:S(2)}) %all-to-all-start.6) | async-done | bytes 98336 | tf_op jit(solution)/shard_map/all_to_all | solution.py:27
  145.8 6.8 %all_to_all.128 = f32[2,64,2,192]{3,2,1,0:T(2,128)S(1)} all-to-all(f32[2,64,2,192]{3,2,1,0:T(2,128)S(1)} %broadcast_in_dim.85), channel_id=1, replica_groups=mesh['sub_0'=8,'sub_1'=8,'sub_2'=2,'grp'=4] {'sub_2'}, dimensions={0} | all-to-all | bytes 393216 | tf_op jit(solution)/shard_map/all_to_all | solution.py:27
  153.0 1.2 fusion.73
  154.2 14.6 %all_to_all.129 = bf16[4,512,192]{1,2,0:T(8,128)(2,1)S(1)} all-to-all(bf16[4,512,192]{1,2,0:T(8,128)(2,1)S(1)} %broadcast_in_dim.86), channel_id=1, replica_groups=mesh['sub_0'=8,'sub_1'=8,'sub_2'=2,'grp'=4] {'grp'}, dimensions={0} | all-to-all | bytes 1572864 | tf_op jit(solution)/shard_map/all_to_all | solution.py:27
  170.7 7.5 %all_to_all.130 = bf16[4,2,12288]{2,1,0:T(2,128)(2,1)S(1)} all-to-all(bf16[4,2,12288]{2,1,0:T(2,128)(2,1)S(1)} %reshape.345), channel_id=1, replica_groups=mesh['sub_0'=8,'sub_1'=8,'sub_2'=2,'grp'=4] {'grp'}, dimensions={0} | all-to-all | bytes 393216 | tf_op jit(solution)/shard_map/all_to_all | solution.py:158
  179.9 2.2 collective-permute-start.10
  182.1 3.1 %collective-permute-start.14 = (bf16[8,3072]{1,0:T(8,128)(2,1)S(1)}, bf16[8,3072]{1,0:T(8,128)(2,1)S(1)}, u32[]{:S(2)}, u32[]{:S(2)}) collective-permute-start(bf16[8,3072]{1,0:T(8,128)(2,1)S(1)} %get-tuple-element.14), channel_id=1, source_target_pairs={{0,8},{4,12},{8,16},{12,20},{16,24},{20,28},{24,32},{28,36},{32,40... | collective-permute-start | bytes 147464 | tf_op jit(solution)/shard_map/ppermute | solution.py:37
  185.2 5.1 %collective-permute-start.13 = (bf16[8,3072]{1,0:T(8,128)(2,1)S(1)}, bf16[8,3072]{1,0:T(8,128)(2,1)S(1)}, u32[]{:S(2)}, u32[]{:S(2)}) collective-permute-start(bf16[8,3072]{1,0:T(8,128)(2,1)S(1)} %get-tuple-element.15), channel_id=1, source_target_pairs={{0,4},{4,8},{8,12},{12,16},{16,20},{20,24},{24,28},{28,32},{32,36}... | collective-permute-start | bytes 147464 | tf_op jit(solution)/shard_map/ppermute | solution.py:37
  190.3 1.9 collective-permute-start.11
  192.3 3.8 %collective-permute-done.11 = bf16[8,3072]{1,0:T(8,128)(2,1)S(1)} collective-permute-done((bf16[8,3072]{1,0:T(8,128)(2,1)S(1)}, bf16[8,3072]{1,0:T(8,128)(2,1)S(1)}, u32[]{:S(2)}, u32[]{:S(2)}) %collective-permute-start.11) | collective-permute-done | bytes 49184 | tf_op jit(solution)/shard_map/ppermute | solution.py:37
  198.9 2.0 collective-permute-start.15
  200.9 9.2 %collective-permute-start.19 = (bf16[8,3072]{1,0:T(8,128)(2,1)S(1)}, bf16[8,3072]{1,0:T(8,128)(2,1)S(1)}, u32[]{:S(2)}, u32[]{:S(2)}) collective-permute-start(bf16[8,3072]{1,0:T(8,128)(2,1)S(1)} %get-tuple-element.9), channel_id=1, source_target_pairs={{0,504},{4,508},{8,0},{12,4},{16,8},{20,12},{24,16},{28,20},{32,24... | collective-permute-start | bytes 147464 | tf_op jit(solution)/shard_map/ppermute | solution.py:37
  210.1 2.5 collective-permute-start.18
  212.7 3.0 %collective-permute-start.16 = (bf16[8,3072]{1,0:T(8,128)(2,1)S(1)}, bf16[8,3072]{1,0:T(8,128)(2,1)S(1)}, u32[]{:S(2)}, u32[]{:S(2)}) collective-permute-start(bf16[8,3072]{1,0:T(8,128)(2,1)S(1)} %get-tuple-element.12), channel_id=1, source_target_pairs={{0,4},{4,8},{8,12},{12,16},{16,20},{20,24},{24,28},{28,32},{32,36}... | collective-permute-start | bytes 147464 | tf_op jit(solution)/shard_map/ppermute | solution.py:37
  215.7 1.1 collective-permute-done.16
  218.3 7.5 %all_to_all.131 = bf16[4,2,12288]{2,1,0:T(2,128)(2,1)S(1)} all-to-all(bf16[4,2,12288]{2,1,0:T(2,128)(2,1)S(1)} %reshape.347), channel_id=1, replica_groups=mesh['sub_0'=8,'sub_1'=8,'sub_2'=2,'grp'=4] {'grp'}, dimensions={0} | all-to-all | bytes 393216 | tf_op jit(solution)/shard_map/all_to_all | solution.py:184
  226.9 6.7 %all_to_all.132 = f32[4,8,192]{2,1,0:T(8,128)S(1)} all-to-all(f32[4,8,192]{2,1,0:T(8,128)S(1)} %broadcast_in_dim.87), channel_id=1, replica_groups=mesh['sub_0'=8,'sub_1'=8,'sub_2'=2,'grp'=4] {'grp'}, dimensions={0} | all-to-all | bytes 49152 | tf_op jit(solution)/shard_map/all_to_all | solution.py:27
  233.9 11.6 %all_to_all.133 = f32[2,64,2,192]{3,1,2,0:T(8,128)S(1)} all-to-all(f32[2,64,2,192]{3,1,2,0:T(8,128)S(1)} %convolution_bitcast_fusion), channel_id=1, replica_groups=mesh['sub_0'=8,'sub_1'=8,'sub_2'=2,'grp'=4] {'sub_2'}, dimensions={0} | all-to-all | bytes 393216 | tf_op jit(solution)/shard_map/all_to_all | solution.py:62
  245.7 15.4 %all_to_all.134 = f32[64,2,192]{2,1,0:T(2,128)S(1)} all-to-all(f32[64,2,192]{2,1,0:T(2,128)S(1)} %copy.185), channel_id=1, replica_groups=mesh['sub_0'=8,'sub_1'=8,'sub_2'=2,'grp'=4] {'sub_0','sub_1'}, dimensions={0} | all-to-all | bytes 196608 | tf_op jit(solution)/shard_map/all_to_all | solution.py:70
  261.9 4.6 %all-to-all-start.14 = ((f32[64,2,192]{2,1,0:T(2,128)}), f32[64,2,192]{2,1,0:T(2,128)S(1)}, u32[]{:S(2)}, u32[]{:S(2)}) async-start(f32[64,2,192]{2,1,0:T(2,128)} %broadcast_in_dim.88), calls=%async_computation.14 | async-start | bytes 262144 | tf_op jit(solution)/shard_map/all_to_all | solution.py:27
  266.7 11.4 %all-to-all-done.14 = f32[64,2,192]{2,1,0:T(2,128)S(1)} async-done(((f32[64,2,192]{2,1,0:T(2,128)}), f32[64,2,192]{2,1,0:T(2,128)S(1)}, u32[]{:S(2)}, u32[]{:S(2)}) %all-to-all-start.14) | async-done | bytes 98336 | tf_op jit(solution)/shard_map/all_to_all | solution.py:27
  278.2 6.7 %all_to_all.135 = f32[2,64,2,192]{3,2,1,0:T(2,128)S(1)} all-to-all(f32[2,64,2,192]{3,2,1,0:T(2,128)S(1)} %broadcast_in_dim.89), channel_id=1, replica_groups=mesh['sub_0'=8,'sub_1'=8,'sub_2'=2,'grp'=4] {'sub_2'}, dimensions={0} | all-to-all | bytes 393216 | tf_op jit(solution)/shard_map/all_to_all | solution.py:27
  285.3 1.2 fusion.6
  (194 shorter events, 33.6 us)
Async XLA Ops:
  0.0 19.4 %copy-start = (bf16[1,512,2048]{2,1,0:T(8,128)(2,1)S(1)}, bf16[1,512,2048]{2,1,0:T(8,128)(2,1)}, u32[]{:S(2)}) copy-start(bf16[1,512,2048]{2,1,0:T(8,128)(2,1)} %param.14) | copy-start | bytes 6291460
  0.0 7.7 %copy-start.22 = (s32[128]{0:T(128)S(1)}, s32[128]{0:T(128)}, u32[]{:S(2)}) copy-start(s32[128]{0:T(128)} %param.22) | copy-start | bytes 1540
  0.0 8.2 %copy-start.8 = (s32[128,32,1]{0,2,1:T(1,128)S(1)}, s32[128,32,1]{0,2,1:T(1,128)}, u32[]{:S(2)}) copy-start(s32[128,32,1]{0,2,1:T(1,128)} %param.19) | copy-start | bytes 49156
  0.0 8.3 %copy-start.9 = (s32[128,32]{0,1:T(8,128)S(1)}, s32[128,32]{0,1:T(8,128)}, u32[]{:S(2)}) copy-start(s32[128,32]{0,1:T(8,128)} %param.20) | copy-start | bytes 49156
  2.2 14.3 %copy-start.12 = (s32[128,16]{0,1:T(8,128)S(1)}, s32[128,16]{0,1:T(8,128)}, u32[]{:S(2)}) copy-start(s32[128,16]{0,1:T(8,128)} %param.21) | copy-start | bytes 24580
  2.2 17.1 %all-to-all-start = ((bf16[4,512,192]{1,2,0:T(8,128)(2,1)}), bf16[4,512,192]{1,2,0:T(8,128)(2,1)S(1)}, u32[]{:S(2)}, u32[]{:S(2)}) async-start(bf16[4,512,192]{1,2,0:T(8,128)(2,1)} %broadcast_in_dim.48), calls=%async_computation | async-start | bytes 1572864 | tf_op jit(solution)/shard_map/all_to_all | solution.py:27
  7.1 12.3 %copy-start.3 = (f32[1,512,192]{1,2,0:T(8,128)S(1)}, f32[1,512,192]{1,2,0:T(8,128)}, u32[]{:S(2)}) copy-start(f32[1,512,192]{1,2,0:T(8,128)} %param.15) | copy-start | bytes 1179652
  8.5 6.2 %copy-start.14 = (s32[1024]{0:T(1024)}, s32[1024]{0:T(1024)S(1)}, u32[]{:S(2)}) copy-start(s32[1024]{0:T(1024)S(1)} %get-tuple-element.37) | copy-start | bytes 12292
  19.3 38.9 %copy-start.6 = (bf16[5,8,16]{2,1,0:T(8,128)(2,1)}, bf16[5,8,16]{2,1,0:T(8,128)(2,1)S(1)}, u32[]{:S(2)}) copy-start(bf16[5,8,16]{2,1,0:T(8,128)(2,1)S(1)} %convolution_convert_fusion.8) | copy-start | bytes 3844
  20.3 5.9 %copy-start.17 = (s32[16]{0:T(128)S(1)}, s32[16]{0:T(128)}, u32[]{:S(2)}) copy-start(s32[16]{0:T(128)} %dynamic-slice_reduce_fusion) | copy-start | bytes 196
  20.3 5.9 %copy-start.20 = (s32[64]{0:T(128)S(1)}, s32[64]{0:T(128)}, u32[]{:S(2)}) copy-start(s32[64]{0:T(128)} %get-tuple-element.35) | copy-start | bytes 772
  20.9 25.7 %copy-start.18 = (pred[5,32]{1,0:T(8,128)(4,1)S(1)}, pred[5,32]{1,0:T(8,128)(4,1)}, u32[]{:S(2)}) copy-start(pred[5,32]{1,0:T(8,128)(4,1)} %get-tuple-element.8) | copy-start | bytes 484
  21.9 9.4 %all-to-all-start.1 = ((bf16[4,2,12288]{2,1,0:T(2,128)(2,1)}), bf16[4,2,12288]{2,1,0:T(2,128)(2,1)S(1)}, u32[]{:S(2)}, u32[]{:S(2)}) async-start(bf16[4,2,12288]{2,1,0:T(2,128)(2,1)} %reshape.341), calls=%async_computation.1 | async-start | bytes 393216 | tf_op jit(solution)/shard_map/all_to_all | solution.py:158
  26.2 55.6 %copy-start.13 = (f32[16,64]{1,0:T(8,128)}, f32[16,64]{1,0:T(8,128)S(1)}, u32[]{:S(2)}) copy-start(f32[16,64]{1,0:T(8,128)S(1)} %and_convert_fusion) | copy-start | bytes 12292
  26.2 53.5 %copy-start.10 = (s32[32]{0:T(128)}, s32[32]{0:T(128)S(1)}, u32[]{:S(2)}) copy-start(s32[32]{0:T(128)S(1)} %fusion.66) | copy-start | bytes 388
  33.0 22.4 %collective-permute-start = (bf16[8,3072]{1,0:T(8,128)(2,1)S(1)}, bf16[8,3072]{1,0:T(8,128)(2,1)S(1)}, u32[]{:S(2)}, u32[]{:S(2)}) collective-permute-start(bf16[8,3072]{1,0:T(8,128)(2,1)S(1)} %get-tuple-element.28), channel_id=1, source_target_pairs={{0,504},{4,508},{8,0},{12,4},{16,8},{20,12},{24,16},{28,20},{32,24... | collective-permute-start | bytes 147464 | tf_op jit(solution)/shard_map/ppermute | solution.py:37
  46.7 11.2 %copy-start.23 = (f32[16]{0:T(128)}, f32[16]{0:T(128)S(1)}, u32[]{:S(2)}) copy-start(f32[16]{0:T(128)S(1)} %fusion.30) | copy-start | bytes 196
  46.7 9.6 %collective-permute-start.4 = (bf16[8,3072]{1,0:T(8,128)(2,1)S(1)}, bf16[8,3072]{1,0:T(8,128)(2,1)S(1)}, u32[]{:S(2)}, u32[]{:S(2)}) collective-permute-start(bf16[8,3072]{1,0:T(8,128)(2,1)S(1)} %get-tuple-element.24), channel_id=1, source_target_pairs={{0,8},{4,12},{8,16},{12,20},{16,24},{20,28},{24,32},{28,36},{32,40... | collective-permute-start | bytes 147464 | tf_op jit(solution)/shard_map/ppermute | solution.py:37
  48.6 7.7 %collective-permute-start.3 = (bf16[8,3072]{1,0:T(8,128)(2,1)S(1)}, bf16[8,3072]{1,0:T(8,128)(2,1)S(1)}, u32[]{:S(2)}, u32[]{:S(2)}) collective-permute-start(bf16[8,3072]{1,0:T(8,128)(2,1)S(1)} %get-tuple-element.25), channel_id=1, source_target_pairs={{0,4},{4,8},{8,12},{12,16},{16,20},{20,24},{24,28},{28,32},{32,36}... | collective-permute-start | bytes 147464 | tf_op jit(solution)/shard_map/ppermute | solution.py:37
  50.5 5.7 %collective-permute-start.2 = (bf16[8,3072]{1,0:T(8,128)(2,1)S(1)}, bf16[8,3072]{1,0:T(8,128)(2,1)S(1)}, u32[]{:S(2)}, u32[]{:S(2)}) collective-permute-start(bf16[8,3072]{1,0:T(8,128)(2,1)S(1)} %get-tuple-element.26), channel_id=1, source_target_pairs={{0,0},{4,4},{8,8},{12,12},{16,16},{20,20},{24,24},{28,28},{32,32},... | collective-permute-start | bytes 147464 | tf_op jit(solution)/shard_map/ppermute | solution.py:37
  50.6 5.7 %collective-permute-start.1 = (bf16[8,3072]{1,0:T(8,128)(2,1)S(1)}, bf16[8,3072]{1,0:T(8,128)(2,1)S(1)}, u32[]{:S(2)}, u32[]{:S(2)}) collective-permute-start(bf16[8,3072]{1,0:T(8,128)(2,1)S(1)} %get-tuple-element.27), channel_id=1, source_target_pairs={{0,508},{4,0},{8,4},{12,8},{16,12},{20,16},{24,20},{28,24},{32,28}... | collective-permute-start | bytes 147464 | tf_op jit(solution)/shard_map/ppermute | solution.py:37
  58.4 26.8 %copy-start.19 = (pred[128]{0:T(512)(128)(4,1)S(1)}, pred[128]{0:T(512)(128)(4,1)}, u32[]{:S(2)}) copy-start(pred[128]{0:T(512)(128)(4,1)} %compare_and_fusion.1) | copy-start | bytes 388
  58.4 27.4 %copy-start.16 = (s32[128,8]{0,1:T(8,128)S(1)}, s32[128,8]{0,1:T(8,128)}, u32[]{:S(2)}) copy-start(s32[128,8]{0,1:T(8,128)} %param.23) | copy-start | bytes 12292
  58.5 20.1 %collective-permute-start.5 = (bf16[8,3072]{1,0:T(8,128)(2,1)S(1)}, bf16[8,3072]{1,0:T(8,128)(2,1)S(1)}, u32[]{:S(2)}, u32[]{:S(2)}) collective-permute-start(bf16[8,3072]{1,0:T(8,128)(2,1)S(1)} %get-tuple-element.23), channel_id=1, source_target_pairs={{0,8},{4,12},{8,16},{12,20},{16,24},{20,28},{24,32},{28,36},{32,40... | collective-permute-start | bytes 147464 | tf_op jit(solution)/shard_map/ppermute | solution.py:37
  60.4 19.3 %collective-permute-start.9 = (bf16[8,3072]{1,0:T(8,128)(2,1)S(1)}, bf16[8,3072]{1,0:T(8,128)(2,1)S(1)}, u32[]{:S(2)}, u32[]{:S(2)}) collective-permute-start(bf16[8,3072]{1,0:T(8,128)(2,1)S(1)} %get-tuple-element.19), channel_id=1, source_target_pairs={{0,504},{4,508},{8,0},{12,4},{16,8},{20,12},{24,16},{28,20},{32,24... | collective-permute-start | bytes 147464 | tf_op jit(solution)/shard_map/ppermute | solution.py:37
  72.9 6.8 %collective-permute-start.8 = (bf16[8,3072]{1,0:T(8,128)(2,1)S(1)}, bf16[8,3072]{1,0:T(8,128)(2,1)S(1)}, u32[]{:S(2)}, u32[]{:S(2)}) collective-permute-start(bf16[8,3072]{1,0:T(8,128)(2,1)S(1)} %get-tuple-element.20), channel_id=1, source_target_pairs={{0,508},{4,0},{8,4},{12,8},{16,12},{20,16},{24,20},{28,24},{32,28}... | collective-permute-start | bytes 147464 | tf_op jit(solution)/shard_map/ppermute | solution.py:37
  75.5 4.2 %collective-permute-start.7 = (bf16[8,3072]{1,0:T(8,128)(2,1)S(1)}, bf16[8,3072]{1,0:T(8,128)(2,1)S(1)}, u32[]{:S(2)}, u32[]{:S(2)}) collective-permute-start(bf16[8,3072]{1,0:T(8,128)(2,1)S(1)} %get-tuple-element.21), channel_id=1, source_target_pairs={{0,0},{4,4},{8,8},{12,12},{16,16},{20,20},{24,24},{28,28},{32,32},... | collective-permute-start | bytes 147464 | tf_op jit(solution)/shard_map/ppermute | solution.py:37
  75.5 4.2 %collective-permute-start.6 = (bf16[8,3072]{1,0:T(8,128)(2,1)S(1)}, bf16[8,3072]{1,0:T(8,128)(2,1)S(1)}, u32[]{:S(2)}, u32[]{:S(2)}) collective-permute-start(bf16[8,3072]{1,0:T(8,128)(2,1)S(1)} %get-tuple-element.22), channel_id=1, source_target_pairs={{0,4},{4,8},{8,12},{12,16},{16,20},{20,24},{24,28},{28,32},{32,36}... | collective-permute-start | bytes 147464 | tf_op jit(solution)/shard_map/ppermute | solution.py:37
  80.8 10.2 %copy-start.5 = (bf16[1,8,512]{2,1,0:T(8,128)(2,1)S(1)}, bf16[1,8,512]{2,1,0:T(8,128)(2,1)}, u32[]{:S(2)}) copy-start(bf16[1,8,512]{2,1,0:T(8,128)(2,1)} %param.18) | copy-start | bytes 24580
  81.8 8.5 %all-to-all-start.2 = ((bf16[4,2,12288]{2,1,0:T(2,128)(2,1)}), bf16[4,2,12288]{2,1,0:T(2,128)(2,1)S(1)}, u32[]{:S(2)}, u32[]{:S(2)}) async-start(bf16[4,2,12288]{2,1,0:T(2,128)(2,1)} %reshape.343), calls=%async_computation.2 | async-start | bytes 393216 | tf_op jit(solution)/shard_map/all_to_all | solution.py:184
  92.0 7.5 %all-to-all-start.3 = ((f32[4,8,192]{2,1,0:T(8,128)}), f32[4,8,192]{2,1,0:T(8,128)S(1)}, u32[]{:S(2)}, u32[]{:S(2)}) async-start(f32[4,8,192]{2,1,0:T(8,128)} %broadcast_in_dim.83), calls=%async_computation.3 | async-start | bytes 65536 | tf_op jit(solution)/shard_map/all_to_all | solution.py:27
  111.6 41.4 %copy-start.1 = (f32[1,512,192]{1,2,0:T(8,128)S(1)}, f32[1,512,192]{1,2,0:T(8,128)}, u32[]{:S(2)}) copy-start(f32[1,512,192]{1,2,0:T(8,128)} %param.16) | copy-start | bytes 1179652
  127.9 16.9 %all-to-all-start.6 = ((f32[64,2,192]{2,1,0:T(2,128)}), f32[64,2,192]{2,1,0:T(2,128)}, u32[]{:S(2)}, u32[]{:S(2)}) async-start(f32[64,2,192]{2,1,0:T(2,128)} %broadcast_in_dim.84), calls=%async_computation.6 | async-start | bytes 262144 | tf_op jit(solution)/shard_map/all_to_all | solution.py:27
  154.1 14.8 %copy-start.4 = (f32[1,512,192]{1,2,0:T(8,128)S(1)}, f32[1,512,192]{1,2,0:T(8,128)}, u32[]{:S(2)}) copy-start(f32[1,512,192]{1,2,0:T(8,128)} %param.15) | copy-start | bytes 1179652
  170.1 9.5 %copy-start.11 = (s32[32]{0:T(128)S(1)}, s32[32]{0:T(128)}, u32[]{:S(2)}) copy-start(s32[32]{0:T(128)} %copy-done.10) | copy-start | bytes 388
  178.9 18.2 %copy-start.7 = (bf16[5,8,16]{2,1,0:T(8,128)(2,1)S(1)}, bf16[5,8,16]{2,1,0:T(8,128)(2,1)}, u32[]{:S(2)}) copy-start(bf16[5,8,16]{2,1,0:T(8,128)(2,1)} %copy-done.6) | copy-start | bytes 3844
  179.9 12.3 %collective-permute-start.10 = (bf16[8,3072]{1,0:T(8,128)(2,1)S(1)}, bf16[8,3072]{1,0:T(8,128)(2,1)S(1)}, u32[]{:S(2)}, u32[]{:S(2)}) collective-permute-start(bf16[8,3072]{1,0:T(8,128)(2,1)S(1)} %get-tuple-element.18), channel_id=1, source_target_pairs={{0,504},{4,508},{8,0},{12,4},{16,8},{20,12},{24,16},{28,20},{32,24... | collective-permute-start | bytes 147464 | tf_op jit(solution)/shard_map/ppermute | solution.py:37
  182.1 14.0 %collective-permute-start.14 = (bf16[8,3072]{1,0:T(8,128)(2,1)S(1)}, bf16[8,3072]{1,0:T(8,128)(2,1)S(1)}, u32[]{:S(2)}, u32[]{:S(2)}) collective-permute-start(bf16[8,3072]{1,0:T(8,128)(2,1)S(1)} %get-tuple-element.14), channel_id=1, source_target_pairs={{0,8},{4,12},{8,16},{12,20},{16,24},{20,28},{24,32},{28,36},{32,40... | collective-permute-start | bytes 147464 | tf_op jit(solution)/shard_map/ppermute | solution.py:37
  185.2 10.8 %collective-permute-start.13 = (bf16[8,3072]{1,0:T(8,128)(2,1)S(1)}, bf16[8,3072]{1,0:T(8,128)(2,1)S(1)}, u32[]{:S(2)}, u32[]{:S(2)}) collective-permute-start(bf16[8,3072]{1,0:T(8,128)(2,1)S(1)} %get-tuple-element.15), channel_id=1, source_target_pairs={{0,4},{4,8},{8,12},{12,16},{16,20},{20,24},{24,28},{28,32},{32,36}... | collective-permute-start | bytes 147464 | tf_op jit(solution)/shard_map/ppermute | solution.py:37
  190.3 5.7 %collective-permute-start.12 = (bf16[8,3072]{1,0:T(8,128)(2,1)S(1)}, bf16[8,3072]{1,0:T(8,128)(2,1)S(1)}, u32[]{:S(2)}, u32[]{:S(2)}) collective-permute-start(bf16[8,3072]{1,0:T(8,128)(2,1)S(1)} %get-tuple-element.16), channel_id=1, source_target_pairs={{0,0},{4,4},{8,8},{12,12},{16,16},{20,20},{24,24},{28,28},{32,32},... | collective-permute-start | bytes 147464 | tf_op jit(solution)/shard_map/ppermute | solution.py:37
  190.3 5.7 %collective-permute-start.11 = (bf16[8,3072]{1,0:T(8,128)(2,1)S(1)}, bf16[8,3072]{1,0:T(8,128)(2,1)S(1)}, u32[]{:S(2)}, u32[]{:S(2)}) collective-permute-start(bf16[8,3072]{1,0:T(8,128)(2,1)S(1)} %get-tuple-element.17), channel_id=1, source_target_pairs={{0,508},{4,0},{8,4},{12,8},{16,12},{20,16},{24,20},{28,24},{32,28}... | collective-permute-start | bytes 147464 | tf_op jit(solution)/shard_map/ppermute | solution.py:37
  198.9 16.8 %collective-permute-start.15 = (bf16[8,3072]{1,0:T(8,128)(2,1)S(1)}, bf16[8,3072]{1,0:T(8,128)(2,1)S(1)}, u32[]{:S(2)}, u32[]{:S(2)}) collective-permute-start(bf16[8,3072]{1,0:T(8,128)(2,1)S(1)} %get-tuple-element.13), channel_id=1, source_target_pairs={{0,8},{4,12},{8,16},{12,20},{16,24},{20,28},{24,32},{28,36},{32,40... | collective-permute-start | bytes 147464 | tf_op jit(solution)/shard_map/ppermute | solution.py:37
  200.9 16.0 %collective-permute-start.19 = (bf16[8,3072]{1,0:T(8,128)(2,1)S(1)}, bf16[8,3072]{1,0:T(8,128)(2,1)S(1)}, u32[]{:S(2)}, u32[]{:S(2)}) collective-permute-start(bf16[8,3072]{1,0:T(8,128)(2,1)S(1)} %get-tuple-element.9), channel_id=1, source_target_pairs={{0,504},{4,508},{8,0},{12,4},{16,8},{20,12},{24,16},{28,20},{32,24... | collective-permute-start | bytes 147464 | tf_op jit(solution)/shard_map/ppermute | solution.py:37
  210.1 6.8 %collective-permute-start.18 = (bf16[8,3072]{1,0:T(8,128)(2,1)S(1)}, bf16[8,3072]{1,0:T(8,128)(2,1)S(1)}, u32[]{:S(2)}, u32[]{:S(2)}) collective-permute-start(bf16[8,3072]{1,0:T(8,128)(2,1)S(1)} %get-tuple-element.10), channel_id=1, source_target_pairs={{0,508},{4,0},{8,4},{12,8},{16,12},{20,16},{24,20},{28,24},{32,28}... | collective-permute-start | bytes 147464 | tf_op jit(solution)/shard_map/ppermute | solution.py:37
  212.7 4.2 %collective-permute-start.17 = (bf16[8,3072]{1,0:T(8,128)(2,1)S(1)}, bf16[8,3072]{1,0:T(8,128)(2,1)S(1)}, u32[]{:S(2)}, u32[]{:S(2)}) collective-permute-start(bf16[8,3072]{1,0:T(8,128)(2,1)S(1)} %get-tuple-element.11), channel_id=1, source_target_pairs={{0,0},{4,4},{8,8},{12,12},{16,16},{20,20},{24,24},{28,28},{32,32},... | collective-permute-start | bytes 147464 | tf_op jit(solution)/shard_map/ppermute | solution.py:37
  212.7 4.2 %collective-permute-start.16 = (bf16[8,3072]{1,0:T(8,128)(2,1)S(1)}, bf16[8,3072]{1,0:T(8,128)(2,1)S(1)}, u32[]{:S(2)}, u32[]{:S(2)}) collective-permute-start(bf16[8,3072]{1,0:T(8,128)(2,1)S(1)} %get-tuple-element.12), channel_id=1, source_target_pairs={{0,4},{4,8},{8,12},{12,16},{16,20},{20,24},{24,28},{28,32},{32,36}... | collective-permute-start | bytes 147464 | tf_op jit(solution)/shard_map/ppermute | solution.py:37
  245.6 39.7 %copy-start.2 = (f32[512,192]{0,1:T(8,128)S(1)}, f32[512,192]{0,1:T(8,128)}, u32[]{:S(2)}) copy-start(f32[512,192]{0,1:T(8,128)} %get-tuple-element.34) | copy-start | bytes 1179652
  261.9 16.2 %all-to-all-start.14 = ((f32[64,2,192]{2,1,0:T(2,128)}), f32[64,2,192]{2,1,0:T(2,128)S(1)}, u32[]{:S(2)}, u32[]{:S(2)}) async-start(f32[64,2,192]{2,1,0:T(2,128)} %broadcast_in_dim.88), calls=%async_computation.14 | async-start | bytes 262144 | tf_op jit(solution)/shard_map/all_to_all | solution.py:27
  (2 other events, 6.5 us)
where the time goes:
time: 288 us; the launch traced here: 286 us
  blocking collectives  104 us (36%)
  starting transfers between devices  97.3 us (34%)
  waiting for transfers between devices  41.8 us (15%)
  local copies, waits for them, and re-layouts  24.6 us (9%)
  matrix products  10.3 us (4%)
  other arithmetic  7.34 us (3%)
    ppermute x20, starting transfers between devices, passed_along(): return lax.ppermute(value, axis, pairs)  71.4 us
    all_to_all x4, blocking collectives, sent_to_all(): return lax.all_to_all(copies, axis, split_axis=0, concat_axis=0, tiled=True)  34.8 us
    all_to_all x2, blocking collectives, summed_rows(): lax.all_to_all(nearer, far, split_axis=0, concat_axis=0, tiled=True)  30.9 us
    all_to_all x4, waiting for transfers between devices, sent_to_all(): return lax.all_to_all(copies, axis, split_axis=0, concat_axis=0, tiled=True)  26.2 us
    all_to_all x2, blocking collectives, sent_and_summed(): lax.all_to_all(parts, axis, split_axis=0, concat_axis=0, tiled=True)  23.3 us
    all_to_all x4, starting transfers between devices, sent_to_all(): return lax.all_to_all(copies, axis, split_axis=0, concat_axis=0, tiled=True)  18.3 us
    all_to_all x1, blocking collectives, body(): lax.all_to_all(coeffs, 'grp', split_axis=2, concat_axis=0, tiled=True)  7.54 us
    all_to_all x1, blocking collectives, body(): lax.all_to_all(own_back.reshape(all_faces, MODES, part_rhs), 'grp', split...  7.54 us
  transfers between devices with their start and end apart: 26, of which 9 were waited for; matrix products, arithmetic and copies ran while one was open for 5% of the time, Pallas kernels for 0%

commit v1 on v0

--- a/solution.py
+++ b/solution.py
@@ -14,6 +14,25 @@
 SUB = ("sub_0", "sub_1", "sub_2")
 relax_weight = 0.5
 coarse_weight = 0.5
+
+
+def review_shelves(piece_in, dim_k, axis_k):
+    comm_axis = "grp"
+    e_now = lax.axis_size(comm_axis)
+    t_next = lax.axis_index(comm_axis)
+    formed, response = (e_now, t_next)
+    opened = piece_in.shape[axis_k] // formed
+    current_value = jnp.roll(piece_in, -response * opened, axis=axis_k)
+    work_now = lax.slice_in_dim(current_value, 0, opened, axis=axis_k)
+    nodes = [work_now]
+    for src_i in tuple(range(1, formed)):
+        r_now = lax.slice_in_dim(current_value, src_i * opened, (src_i + 1) * opened, axis=axis_k)
+        val = lax.ppermute(
+            r_now, comm_axis, [(to_i, (to_i + src_i) % formed) for to_i in range(formed)]
+        )
+        nodes.append(val)
+    tall = jnp.concatenate(nodes[::-1], axis=dim_k)
+    return jnp.roll(tall, (response + 1) * nodes[0].shape[dim_k], axis=dim_k)
 
 
 def joined_along(parts, dim):
@@ -155,7 +174,7 @@
         coeffs = jnp.einsum(
             "fmp,fpr->fmr", tables, face_res, preferred_element_type=jnp.float32
         ).astype(jnp.bfloat16)
-        grouped = lax.all_to_all(coeffs, "grp", split_axis=2, concat_axis=0, tiled=True)
+        grouped = review_shelves(coeffs, 0, 2)
         part_rhs = grouped.shape[2]
         payload = grouped.reshape(all_faces, MODES * part_rhs)
         outgoing = jnp.dot(send_table, payload, preferred_element_type=jnp.float32).astype(

time: 288 us -> 301 us (1.045)
  starting transfers between devices: 97.3 us -> 112 us
  blocking collectives: 104 us -> 97.7 us
  other arithmetic: 7.34 us -> 10.8 us
    ppermute x0 -> x6, starting transfers between devices: none -> 19.2 us  [review_shelves(): lax.ppermute(r_now, comm_axis, [(to_i, (to_i + src_i) % formed) for to_i...]
    all_to_all x1 -> x0, blocking collectives: 7.54 us -> none  [body(): lax.all_to_all(coeffs, 'grp', split_axis=2, concat_axis=0, tiled=True)]
    ppermute x0 -> x6, waiting for transfers between devices: none -> 7.51 us  [review_shelves(): lax.ppermute(r_now, comm_axis, [(to_i, (to_i + src_i) % formed) for to_i...]
    all_to_all x1 -> x0, waiting for transfers between devices: 5.07 us -> none  [body(): lax.all_to_all(coeffs, 'grp', split_axis=2, concat_axis=0, tiled=True)]
    all_to_all x1 -> x0, starting transfers between devices: 4.24 us -> none  [body(): lax.all_to_all(coeffs, 'grp', split_axis=2, concat_axis=0, tiled=True)]
    concatenate x0 -> x4, other arithmetic: none -> 3.38 us  [the longest x2 2.79 us: review_shelves(): return jnp.roll(tall, (response + 1) * nodes[0].shape[dim_k], axis=dim_k)]
  transfers between devices with their start and end apart: 26 -> 31, of which waited for: 9 -> 11; matrix products, arithmetic and copies ran while one was open for 5% -> 5% of each run, Pallas kernels for 0% -> 0%
where the time goes in v1:
time: 301 us; the launch traced here: 299 us
  starting transfers between devices  112 us (37%)
  blocking collectives  97.7 us (32%)
  waiting for transfers between devices  44.1 us (15%)
  local copies, waits for them, and re-layouts  22.6 us (8%)
  matrix products  10.9 us (4%)
  other arithmetic  10.8 us (4%)
    ppermute x20, starting transfers between devices, passed_along(): return lax.ppermute(value, axis, pairs)  70.9 us
    all_to_all x4, blocking collectives, sent_to_all(): return lax.all_to_all(copies, axis, split_axis=0, concat_axis=0, tiled=True)  34.7 us
    all_to_all x2, blocking collectives, summed_rows(): lax.all_to_all(nearer, far, split_axis=0, concat_axis=0, tiled=True)  30.9 us
    all_to_all x4, waiting for transfers between devices, sent_to_all(): return lax.all_to_all(copies, axis, split_axis=0, concat_axis=0, tiled=True)  26 us
    all_to_all x2, blocking collectives, sent_and_summed(): lax.all_to_all(parts, axis, split_axis=0, concat_axis=0, tiled=True)  23.9 us
    ppermute x6, starting transfers between devices, review_shelves(): lax.ppermute(r_now, comm_axis, [(to_i, (to_i + src_i) % formed) for to_i...  19.2 us
    all_to_all x4, starting transfers between devices, sent_to_all(): return lax.all_to_all(copies, axis, split_axis=0, concat_axis=0, tiled=True)  18.3 us
    all_to_all x1, blocking collectives, body(): lax.all_to_all(own_back.reshape(all_faces, MODES, part_rhs), 'grp', split...  8.32 us
  transfers between devices with their start and end apart: 31, of which 11 were waited for; matrix products, arithmetic and copies ran while one was open for 5% of the time, Pallas kernels for 0%

profile of v1, /device:TPU:1, one launch (start us, length us, event | category | flops | bytes accessed | tf_op | source)
XLA Modules:
  0.0 299.4 jit_solution(7571470210966388886)
XLA Ops:
  2.2 4.8 %all-to-all-start = ((bf16[4,512,192]{1,2,0:T(8,128)(2,1)}), bf16[4,512,192]{1,2,0:T(8,128)(2,1)S(1)}, u32[]{:S(2)}, u32[]{:S(2)}) async-start(bf16[4,512,192]{1,2,0:T(8,128)(2,1)} %broadcast_in_dim.48), calls=%async_computation | async-start | bytes 1572864 | tf_op jit(solution)/shard_map/all_to_all | solution.py:46
  11.0 1.4 gather_fusion.4
  15.2 1.3 and_convert_fusion
  16.5 1.3 fusion.84
  21.1 3.4 %collective-permute-start.2 = (bf16[8,64,48]{2,1,0:T(8,128)(2,1)S(1)}, bf16[8,64,48]{2,1,0:T(8,128)(2,1)S(1)}, u32[]{:S(2)}, u32[]{:S(2)}) collective-permute-start(bf16[8,64,48]{2,1,0:T(8,128)(2,1)S(1)} %get-tuple-element.16), channel_id=1, source_target_pairs={{0,1},{1,2},{2,3},{3,0},{4,5},{5,6},{6,7},{7,4},{8,9},{9,10},{10,1... | collective-permute-start | bytes 147464 | tf_op jit(solution)/shard_map/ppermute | solution.py:30
  24.4 4.3 %collective-permute-start.1 = (bf16[8,64,48]{2,1,0:T(8,128)(2,1)S(1)}, bf16[8,64,48]{2,1,0:T(8,128)(2,1)S(1)}, u32[]{:S(2)}, u32[]{:S(2)}) collective-permute-start(bf16[8,64,48]{2,1,0:T(8,128)(2,1)S(1)} %get-tuple-element.17), channel_id=1, source_target_pairs={{0,2},{1,3},{2,0},{3,1},{4,6},{5,7},{6,4},{7,5},{8,10},{9,11},{10,... | collective-permute-start | bytes 147464 | tf_op jit(solution)/shard_map/ppermute | solution.py:30
  28.7 3.1 %collective-permute-start = (bf16[8,64,48]{2,1,0:T(8,128)(2,1)S(1)}, bf16[8,64,48]{2,1,0:T(8,128)(2,1)}, u32[]{:S(2)}, u32[]{:S(2)}) collective-permute-start(bf16[8,64,48]{2,1,0:T(8,128)(2,1)S(1)} %get-tuple-element.18), channel_id=1, source_target_pairs={{0,3},{1,0},{2,1},{3,2},{4,7},{5,4},{6,5},{7,6},{8,11},{9,8},{10,9... | collective-permute-start | bytes 147464 | tf_op jit(solution)/shard_map/ppermute | solution.py:30
  31.9 2.6 collective-permute-done
  34.6 1.8 fusion.41
  37.4 13.6 %collective-permute-start.3 = (bf16[8,3072]{1,0:T(8,128)(2,1)S(1)}, bf16[8,3072]{1,0:T(8,128)(2,1)S(1)}, u32[]{:S(2)}, u32[]{:S(2)}) collective-permute-start(bf16[8,3072]{1,0:T(8,128)(2,1)S(1)} %get-tuple-element.38), channel_id=1, source_target_pairs={{0,504},{4,508},{8,0},{12,4},{16,8},{20,12},{24,16},{28,20},{32,24... | collective-permute-start | bytes 147464 | tf_op jit(solution)/shard_map/ppermute | solution.py:56
  51.9 1.9 collective-permute-start.7
  53.8 1.9 collective-permute-start.6
  55.7 5.1 %collective-permute-start.4 = (bf16[8,3072]{1,0:T(8,128)(2,1)S(1)}, bf16[8,3072]{1,0:T(8,128)(2,1)S(1)}, u32[]{:S(2)}, u32[]{:S(2)}) collective-permute-start(bf16[8,3072]{1,0:T(8,128)(2,1)S(1)} %get-tuple-element.37), channel_id=1, source_target_pairs={{0,508},{4,0},{8,4},{12,8},{16,12},{20,16},{24,20},{28,24},{32,28}... | collective-permute-start | bytes 147464 | tf_op jit(solution)/shard_map/ppermute | solution.py:56
  63.9 1.9 collective-permute-start.8
  65.8 12.5 %collective-permute-start.12 = (bf16[8,3072]{1,0:T(8,128)(2,1)S(1)}, bf16[8,3072]{1,0:T(8,128)(2,1)S(1)}, u32[]{:S(2)}, u32[]{:S(2)}) collective-permute-start(bf16[8,3072]{1,0:T(8,128)(2,1)S(1)} %get-tuple-element.29), channel_id=1, source_target_pairs={{0,504},{4,508},{8,0},{12,4},{16,8},{20,12},{24,16},{28,20},{32,24... | collective-permute-start | bytes 147464 | tf_op jit(solution)/shard_map/ppermute | solution.py:56
  78.4 2.5 collective-permute-start.11
  80.9 3.0 %collective-permute-start.9 = (bf16[8,3072]{1,0:T(8,128)(2,1)S(1)}, bf16[8,3072]{1,0:T(8,128)(2,1)S(1)}, u32[]{:S(2)}, u32[]{:S(2)}) collective-permute-start(bf16[8,3072]{1,0:T(8,128)(2,1)S(1)} %get-tuple-element.32), channel_id=1, source_target_pairs={{0,4},{4,8},{8,12},{12,16},{16,20},{20,24},{24,28},{28,32},{32,36}... | collective-permute-start | bytes 147464 | tf_op jit(solution)/shard_map/ppermute | solution.py:56
  87.3 3.7 %all-to-all-start.1 = ((bf16[4,2,12288]{2,1,0:T(2,128)(2,1)}), bf16[4,2,12288]{2,1,0:T(2,128)(2,1)S(1)}, u32[]{:S(2)}, u32[]{:S(2)}) async-start(bf16[4,2,12288]{2,1,0:T(2,128)(2,1)} %reshape.339), calls=%async_computation.1 | async-start | bytes 393216 | tf_op jit(solution)/shard_map/all_to_all | solution.py:203
  92.4 3.7 %all-to-all-done.1 = bf16[4,2,12288]{2,1,0:T(2,128)(2,1)S(1)} async-done(((bf16[4,2,12288]{2,1,0:T(2,128)(2,1)}), bf16[4,2,12288]{2,1,0:T(2,128)(2,1)S(1)}, u32[]{:S(2)}, u32[]{:S(2)}) %all-to-all-start.1) | async-done | bytes 196640 | tf_op jit(solution)/shard_map/all_to_all | solution.py:203
  97.8 3.3 %all-to-all-start.2 = ((f32[4,8,192]{2,1,0:T(8,128)}), f32[4,8,192]{2,1,0:T(8,128)S(1)}, u32[]{:S(2)}, u32[]{:S(2)}) async-start(f32[4,8,192]{2,1,0:T(8,128)} %broadcast_in_dim.83), calls=%async_computation.2 | async-start | bytes 65536 | tf_op jit(solution)/shard_map/all_to_all | solution.py:46
  101.7 3.6 %all-to-all-done.2 = f32[4,8,192]{2,1,0:T(8,128)S(1)} async-done(((f32[4,8,192]{2,1,0:T(8,128)}), f32[4,8,192]{2,1,0:T(8,128)S(1)}, u32[]{:S(2)}, u32[]{:S(2)}) %all-to-all-start.2) | async-done | bytes 24608 | tf_op jit(solution)/shard_map/all_to_all | solution.py:46
  105.7 11.9 %all_to_all.96 = f32[2,64,2,192]{3,1,2,0:T(8,128)S(1)} all-to-all(f32[2,64,2,192]{3,1,2,0:T(8,128)S(1)} %convolution_bitcast_fusion.1), channel_id=1, replica_groups=mesh['sub_0'=8,'sub_1'=8,'sub_2'=2,'grp'=4] {'sub_2'}, dimensions={0} | all-to-all | bytes 393216 | tf_op jit(solution)/shard_map/all_to_all | solution.py:81
  117.8 15.4 %all_to_all.97 = f32[64,2,192]{2,1,0:T(2,128)S(1)} all-to-all(f32[64,2,192]{2,1,0:T(2,128)S(1)} %copy.145), channel_id=1, replica_groups=mesh['sub_0'=8,'sub_1'=8,'sub_2'=2,'grp'=4] {'sub_0','sub_1'}, dimensions={0} | all-to-all | bytes 196608 | tf_op jit(solution)/shard_map/all_to_all | solution.py:89
  134.0 5.6 %all-to-all-start.5 = ((f32[64,2,192]{2,1,0:T(2,128)}), f32[64,2,192]{2,1,0:T(2,128)}, u32[]{:S(2)}, u32[]{:S(2)}) async-start(f32[64,2,192]{2,1,0:T(2,128)} %broadcast_in_dim.84), calls=%async_computation.5 | async-start | bytes 262144 | tf_op jit(solution)/shard_map/all_to_all | solution.py:46
  139.8 11.0 %all-to-all-done.5 = f32[64,2,192]{2,1,0:T(2,128)} async-done(((f32[64,2,192]{2,1,0:T(2,128)}), f32[64,2,192]{2,1,0:T(2,128)}, u32[]{:S(2)}, u32[]{:S(2)}) %all-to-all-start.5) | async-done | bytes 98336 | tf_op jit(solution)/shard_map/all_to_all | solution.py:46
  151.8 6.7 %all_to_all.98 = f32[2,64,2,192]{3,2,1,0:T(2,128)S(1)} all-to-all(f32[2,64,2,192]{3,2,1,0:T(2,128)S(1)} %broadcast_in_dim.85), channel_id=1, replica_groups=mesh['sub_0'=8,'sub_1'=8,'sub_2'=2,'grp'=4] {'sub_2'}, dimensions={0} | all-to-all | bytes 393216 | tf_op jit(solution)/shard_map/all_to_all | solution.py:46
  160.2 14.6 %all_to_all.99 = bf16[4,512,192]{1,2,0:T(8,128)(2,1)S(1)} all-to-all(bf16[4,512,192]{1,2,0:T(8,128)(2,1)S(1)} %broadcast_in_dim.86), channel_id=1, replica_groups=mesh['sub_0'=8,'sub_1'=8,'sub_2'=2,'grp'=4] {'grp'}, dimensions={0} | all-to-all | bytes 1572864 | tf_op jit(solution)/shard_map/all_to_all | solution.py:46
  176.5 2.2 collective-permute-start.15
  178.8 3.7 %collective-permute-start.14 = (bf16[8,64,48]{2,1,0:T(8,128)(2,1)S(1)}, bf16[8,64,48]{2,1,0:T(8,128)(2,1)S(1)}, u32[]{:S(2)}, u32[]{:S(2)}) collective-permute-start(bf16[8,64,48]{2,1,0:T(8,128)(2,1)S(1)} %get-tuple-element.13), channel_id=1, source_target_pairs={{0,2},{1,3},{2,0},{3,1},{4,6},{5,7},{6,4},{7,5},{8,10},{9,11},{10,... | collective-permute-start | bytes 147464 | tf_op jit(solution)/shard_map/ppermute | solution.py:30
  182.4 2.5 collective-permute-start.13
  186.1 3.8 %collective-permute-done.13 = bf16[8,64,48]{2,1,0:T(8,128)(2,1)S(1)} collective-permute-done((bf16[8,64,48]{2,1,0:T(8,128)(2,1)S(1)}, bf16[8,64,48]{2,1,0:T(8,128)(2,1)S(1)}, u32[]{:S(2)}, u32[]{:S(2)}) %collective-permute-start.13) | collective-permute-done | bytes 49184 | tf_op jit(solution)/shard_map/ppermute | solution.py:30
  192.5 2.2 collective-permute-start.16
  194.7 3.1 %collective-permute-start.20 = (bf16[8,3072]{1,0:T(8,128)(2,1)S(1)}, bf16[8,3072]{1,0:T(8,128)(2,1)S(1)}, u32[]{:S(2)}, u32[]{:S(2)}) collective-permute-start(bf16[8,3072]{1,0:T(8,128)(2,1)S(1)} %get-tuple-element.24), channel_id=1, source_target_pairs={{0,8},{4,12},{8,16},{12,20},{16,24},{20,28},{24,32},{28,36},{32,40... | collective-permute-start | bytes 147464 | tf_op jit(solution)/shard_map/ppermute | solution.py:56
  197.8 4.3 %collective-permute-start.19 = (bf16[8,3072]{1,0:T(8,128)(2,1)S(1)}, bf16[8,3072]{1,0:T(8,128)(2,1)S(1)}, u32[]{:S(2)}, u32[]{:S(2)}) collective-permute-start(bf16[8,3072]{1,0:T(8,128)(2,1)S(1)} %get-tuple-element.25), channel_id=1, source_target_pairs={{0,4},{4,8},{8,12},{12,16},{16,20},{20,24},{24,28},{28,32},{32,36}... | collective-permute-start | bytes 147464 | tf_op jit(solution)/shard_map/ppermute | solution.py:56
  202.2 1.9 collective-permute-start.17
  204.1 3.8 %collective-permute-done.17 = bf16[8,3072]{1,0:T(8,128)(2,1)S(1)} collective-permute-done((bf16[8,3072]{1,0:T(8,128)(2,1)S(1)}, bf16[8,3072]{1,0:T(8,128)(2,1)S(1)}, u32[]{:S(2)}, u32[]{:S(2)}) %collective-permute-start.17) | collective-permute-done | bytes 49184 | tf_op jit(solution)/shard_map/ppermute | solution.py:56
  210.7 2.0 collective-permute-start.21
  212.8 9.2 %collective-permute-start.25 = (bf16[8,3072]{1,0:T(8,128)(2,1)S(1)}, bf16[8,3072]{1,0:T(8,128)(2,1)S(1)}, u32[]{:S(2)}, u32[]{:S(2)}) collective-permute-start(bf16[8,3072]{1,0:T(8,128)(2,1)S(1)} %get-tuple-element.19), channel_id=1, source_target_pairs={{0,504},{4,508},{8,0},{12,4},{16,8},{20,12},{24,16},{28,20},{32,24... | collective-permute-start | bytes 147464 | tf_op jit(solution)/shard_map/ppermute | solution.py:56
  222.0 2.5 collective-permute-start.24
  224.5 3.0 %collective-permute-start.22 = (bf16[8,3072]{1,0:T(8,128)(2,1)S(1)}, bf16[8,3072]{1,0:T(8,128)(2,1)S(1)}, u32[]{:S(2)}, u32[]{:S(2)}) collective-permute-start(bf16[8,3072]{1,0:T(8,128)(2,1)S(1)} %get-tuple-element.22), channel_id=1, source_target_pairs={{0,4},{4,8},{8,12},{12,16},{16,20},{20,24},{24,28},{28,32},{32,36}... | collective-permute-start | bytes 147464 | tf_op jit(solution)/shard_map/ppermute | solution.py:56
  230.2 8.3 %all_to_all.100 = bf16[4,2,12288]{2,1,0:T(2,128)(2,1)S(1)} all-to-all(bf16[4,2,12288]{2,1,0:T(2,128)(2,1)S(1)} %reshape.341), channel_id=1, replica_groups=mesh['sub_0'=8,'sub_1'=8,'sub_2'=2,'grp'=4] {'grp'}, dimensions={0} | all-to-all | bytes 393216 | tf_op jit(solution)/shard_map/all_to_all | solution.py:203
  239.5 6.7 %all_to_all.101 = f32[4,8,192]{2,1,0:T(8,128)S(1)} all-to-all(f32[4,8,192]{2,1,0:T(8,128)S(1)} %broadcast_in_dim.87), channel_id=1, replica_groups=mesh['sub_0'=8,'sub_1'=8,'sub_2'=2,'grp'=4] {'grp'}, dimensions={0} | all-to-all | bytes 49152 | tf_op jit(solution)/shard_map/all_to_all | solution.py:46
  246.6 11.9 %all_to_all.102 = f32[2,64,2,192]{3,1,2,0:T(8,128)S(1)} all-to-all(f32[2,64,2,192]{3,1,2,0:T(8,128)S(1)} %convolution_bitcast_fusion), channel_id=1, replica_groups=mesh['sub_0'=8,'sub_1'=8,'sub_2'=2,'grp'=4] {'sub_2'}, dimensions={0} | all-to-all | bytes 393216 | tf_op jit(solution)/shard_map/all_to_all | solution.py:81
  258.6 15.4 %all_to_all.103 = f32[64,2,192]{2,1,0:T(2,128)S(1)} all-to-all(f32[64,2,192]{2,1,0:T(2,128)S(1)} %copy.157), channel_id=1, replica_groups=mesh['sub_0'=8,'sub_1'=8,'sub_2'=2,'grp'=4] {'sub_0','sub_1'}, dimensions={0} | all-to-all | bytes 196608 | tf_op jit(solution)/shard_map/all_to_all | solution.py:89
  274.9 4.6 %all-to-all-start.12 = ((f32[64,2,192]{2,1,0:T(2,128)}), f32[64,2,192]{2,1,0:T(2,128)S(1)}, u32[]{:S(2)}, u32[]{:S(2)}) async-start(f32[64,2,192]{2,1,0:T(2,128)} %broadcast_in_dim.88), calls=%async_computation.12 | async-start | bytes 262144 | tf_op jit(solution)/shard_map/all_to_all | solution.py:46
  279.7 11.4 %all-to-all-done.12 = f32[64,2,192]{2,1,0:T(2,128)S(1)} async-done(((f32[64,2,192]{2,1,0:T(2,128)}), f32[64,2,192]{2,1,0:T(2,128)S(1)}, u32[]{:S(2)}, u32[]{:S(2)}) %all-to-all-start.12) | async-done | bytes 98336 | tf_op jit(solution)/shard_map/all_to_all | solution.py:46
  291.1 6.7 %all_to_all.104 = f32[2,64,2,192]{3,2,1,0:T(2,128)S(1)} all-to-all(f32[2,64,2,192]{3,2,1,0:T(2,128)S(1)} %broadcast_in_dim.89), channel_id=1, replica_groups=mesh['sub_0'=8,'sub_1'=8,'sub_2'=2,'grp'=4] {'sub_2'}, dimensions={0} | all-to-all | bytes 393216 | tf_op jit(solution)/shard_map/all_to_all | solution.py:46
  298.2 1.2 fusion.6
  (193 shorter events, 41.6 us)
Async XLA Ops:
  0.0 19.3 %copy-start = (bf16[1,512,2048]{2,1,0:T(8,128)(2,1)S(1)}, bf16[1,512,2048]{2,1,0:T(8,128)(2,1)}, u32[]{:S(2)}) copy-start(bf16[1,512,2048]{2,1,0:T(8,128)(2,1)} %param.18) | copy-start | bytes 6291460
  0.0 7.6 %copy-start.18 = (s32[128]{0:T(128)S(1)}, s32[128]{0:T(128)}, u32[]{:S(2)}) copy-start(s32[128]{0:T(128)} %param.26) | copy-start | bytes 1540
  0.0 8.1 %copy-start.8 = (s32[128,32,1]{0,2,1:T(1,128)S(1)}, s32[128,32,1]{0,2,1:T(1,128)}, u32[]{:S(2)}) copy-start(s32[128,32,1]{0,2,1:T(1,128)} %param.23) | copy-start | bytes 49156
  0.0 8.2 %copy-start.9 = (s32[128,32]{0,1:T(8,128)S(1)}, s32[128,32]{0,1:T(8,128)}, u32[]{:S(2)}) copy-start(s32[128,32]{0,1:T(8,128)} %param.24) | copy-start | bytes 49156
  2.2 17.1 %all-to-all-start = ((bf16[4,512,192]{1,2,0:T(8,128)(2,1)}), bf16[4,512,192]{1,2,0:T(8,128)(2,1)S(1)}, u32[]{:S(2)}, u32[]{:S(2)}) async-start(bf16[4,512,192]{1,2,0:T(8,128)(2,1)} %broadcast_in_dim.48), calls=%async_computation | async-start | bytes 1572864 | tf_op jit(solution)/shard_map/all_to_all | solution.py:46
  7.0 12.4 %copy-start.3 = (f32[1,512,192]{1,2,0:T(8,128)S(1)}, f32[1,512,192]{1,2,0:T(8,128)}, u32[]{:S(2)}) copy-start(f32[1,512,192]{1,2,0:T(8,128)} %param.19) | copy-start | bytes 1179652
  19.2 44.4 %copy-start.6 = (bf16[5,8,16]{2,1,0:T(8,128)(2,1)}, bf16[5,8,16]{2,1,0:T(8,128)(2,1)S(1)}, u32[]{:S(2)}) copy-start(bf16[5,8,16]{2,1,0:T(8,128)(2,1)S(1)} %convolution_convert_fusion.8) | copy-start | bytes 3844
  21.1 10.8 %collective-permute-start.2 = (bf16[8,64,48]{2,1,0:T(8,128)(2,1)S(1)}, bf16[8,64,48]{2,1,0:T(8,128)(2,1)S(1)}, u32[]{:S(2)}, u32[]{:S(2)}) collective-permute-start(bf16[8,64,48]{2,1,0:T(8,128)(2,1)S(1)} %get-tuple-element.16), channel_id=1, source_target_pairs={{0,1},{1,2},{2,3},{3,0},{4,5},{5,6},{6,7},{7,4},{8,9},{9,10},{10,1... | collective-permute-start | bytes 147464 | tf_op jit(solution)/shard_map/ppermute | solution.py:30
  24.4 7.5 %collective-permute-start.1 = (bf16[8,64,48]{2,1,0:T(8,128)(2,1)S(1)}, bf16[8,64,48]{2,1,0:T(8,128)(2,1)S(1)}, u32[]{:S(2)}, u32[]{:S(2)}) collective-permute-start(bf16[8,64,48]{2,1,0:T(8,128)(2,1)S(1)} %get-tuple-element.17), channel_id=1, source_target_pairs={{0,2},{1,3},{2,0},{3,1},{4,6},{5,7},{6,4},{7,5},{8,10},{9,11},{10,... | collective-permute-start | bytes 147464 | tf_op jit(solution)/shard_map/ppermute | solution.py:30
  28.7 5.8 %collective-permute-start = (bf16[8,64,48]{2,1,0:T(8,128)(2,1)S(1)}, bf16[8,64,48]{2,1,0:T(8,128)(2,1)}, u32[]{:S(2)}, u32[]{:S(2)}) collective-permute-start(bf16[8,64,48]{2,1,0:T(8,128)(2,1)S(1)} %get-tuple-element.18), channel_id=1, source_target_pairs={{0,3},{1,0},{2,1},{3,2},{4,7},{5,4},{6,5},{7,6},{8,11},{9,8},{10,9... | collective-permute-start | bytes 147464 | tf_op jit(solution)/shard_map/ppermute | solution.py:30
  31.9 53.3 %copy-start.10 = (s32[32]{0:T(128)}, s32[32]{0:T(128)S(1)}, u32[]{:S(2)}) copy-start(s32[32]{0:T(128)S(1)} %fusion.82) | copy-start | bytes 388
  36.4 26.4 %copy-start.12 = (f32[16,64]{1,0:T(8,128)S(1)}, f32[16,64]{1,0:T(8,128)}, u32[]{:S(2)}) copy-start(f32[16,64]{1,0:T(8,128)} %and_convert_fusion) | copy-start | bytes 12292
  37.4 23.4 %collective-permute-start.3 = (bf16[8,3072]{1,0:T(8,128)(2,1)S(1)}, bf16[8,3072]{1,0:T(8,128)(2,1)S(1)}, u32[]{:S(2)}, u32[]{:S(2)}) collective-permute-start(bf16[8,3072]{1,0:T(8,128)(2,1)S(1)} %get-tuple-element.38), channel_id=1, source_target_pairs={{0,504},{4,508},{8,0},{12,4},{16,8},{20,12},{24,16},{28,20},{32,24... | collective-permute-start | bytes 147464 | tf_op jit(solution)/shard_map/ppermute | solution.py:56
  51.9 11.5 %copy-start.19 = (f32[16]{0:T(128)}, f32[16]{0:T(128)S(1)}, u32[]{:S(2)}) copy-start(f32[16]{0:T(128)S(1)} %fusion.30) | copy-start | bytes 196
  51.9 9.9 %collective-permute-start.7 = (bf16[8,3072]{1,0:T(8,128)(2,1)S(1)}, bf16[8,3072]{1,0:T(8,128)(2,1)S(1)}, u32[]{:S(2)}, u32[]{:S(2)}) collective-permute-start(bf16[8,3072]{1,0:T(8,128)(2,1)S(1)} %get-tuple-element.34), channel_id=1, source_target_pairs={{0,8},{4,12},{8,16},{12,20},{16,24},{20,28},{24,32},{28,36},{32,40... | collective-permute-start | bytes 147464 | tf_op jit(solution)/shard_map/ppermute | solution.py:56
  53.8 8.0 %collective-permute-start.6 = (bf16[8,3072]{1,0:T(8,128)(2,1)S(1)}, bf16[8,3072]{1,0:T(8,128)(2,1)S(1)}, u32[]{:S(2)}, u32[]{:S(2)}) collective-permute-start(bf16[8,3072]{1,0:T(8,128)(2,1)S(1)} %get-tuple-element.35), channel_id=1, source_target_pairs={{0,4},{4,8},{8,12},{12,16},{16,20},{20,24},{24,28},{28,32},{32,36}... | collective-permute-start | bytes 147464 | tf_op jit(solution)/shard_map/ppermute | solution.py:56
  55.7 6.0 %collective-permute-start.5 = (bf16[8,3072]{1,0:T(8,128)(2,1)S(1)}, bf16[8,3072]{1,0:T(8,128)(2,1)S(1)}, u32[]{:S(2)}, u32[]{:S(2)}) collective-permute-start(bf16[8,3072]{1,0:T(8,128)(2,1)S(1)} %get-tuple-element.36), channel_id=1, source_target_pairs={{0,0},{4,4},{8,8},{12,12},{16,16},{20,20},{24,24},{28,28},{32,32},... | collective-permute-start | bytes 147464 | tf_op jit(solution)/shard_map/ppermute | solution.py:56
  55.7 6.0 %collective-permute-start.4 = (bf16[8,3072]{1,0:T(8,128)(2,1)S(1)}, bf16[8,3072]{1,0:T(8,128)(2,1)S(1)}, u32[]{:S(2)}, u32[]{:S(2)}) collective-permute-start(bf16[8,3072]{1,0:T(8,128)(2,1)S(1)} %get-tuple-element.37), channel_id=1, source_target_pairs={{0,508},{4,0},{8,4},{12,8},{16,12},{20,16},{24,20},{28,24},{32,28}... | collective-permute-start | bytes 147464 | tf_op jit(solution)/shard_map/ppermute | solution.py:56
  63.9 27.1 %copy-start.17 = (pred[128]{0:T(512)(128)(4,1)S(1)}, pred[128]{0:T(512)(128)(4,1)}, u32[]{:S(2)}) copy-start(pred[128]{0:T(512)(128)(4,1)} %copy-done.16) | copy-start | bytes 388
  63.9 27.7 %copy-start.14 = (s32[128,8]{0,1:T(8,128)S(1)}, s32[128,8]{0,1:T(8,128)}, u32[]{:S(2)}) copy-start(s32[128,8]{0,1:T(8,128)} %param.27) | copy-start | bytes 12292
  63.9 20.1 %collective-permute-start.8 = (bf16[8,3072]{1,0:T(8,128)(2,1)S(1)}, bf16[8,3072]{1,0:T(8,128)(2,1)S(1)}, u32[]{:S(2)}, u32[]{:S(2)}) collective-permute-start(bf16[8,3072]{1,0:T(8,128)(2,1)S(1)} %get-tuple-element.33), channel_id=1, source_target_pairs={{0,8},{4,12},{8,16},{12,20},{16,24},{20,28},{24,32},{28,36},{32,40... | collective-permute-start | bytes 147464 | tf_op jit(solution)/shard_map/ppermute | solution.py:56
  65.8 19.3 %collective-permute-start.12 = (bf16[8,3072]{1,0:T(8,128)(2,1)S(1)}, bf16[8,3072]{1,0:T(8,128)(2,1)S(1)}, u32[]{:S(2)}, u32[]{:S(2)}) collective-permute-start(bf16[8,3072]{1,0:T(8,128)(2,1)S(1)} %get-tuple-element.29), channel_id=1, source_target_pairs={{0,504},{4,508},{8,0},{12,4},{16,8},{20,12},{24,16},{28,20},{32,24... | collective-permute-start | bytes 147464 | tf_op jit(solution)/shard_map/ppermute | solution.py:56
  78.4 6.8 %collective-permute-start.11 = (bf16[8,3072]{1,0:T(8,128)(2,1)S(1)}, bf16[8,3072]{1,0:T(8,128)(2,1)S(1)}, u32[]{:S(2)}, u32[]{:S(2)}) collective-permute-start(bf16[8,3072]{1,0:T(8,128)(2,1)S(1)} %get-tuple-element.30), channel_id=1, source_target_pairs={{0,508},{4,0},{8,4},{12,8},{16,12},{20,16},{24,20},{28,24},{32,28}... | collective-permute-start | bytes 147464 | tf_op jit(solution)/shard_map/ppermute | solution.py:56
  80.9 4.2 %collective-permute-start.10 = (bf16[8,3072]{1,0:T(8,128)(2,1)S(1)}, bf16[8,3072]{1,0:T(8,128)(2,1)S(1)}, u32[]{:S(2)}, u32[]{:S(2)}) collective-permute-start(bf16[8,3072]{1,0:T(8,128)(2,1)S(1)} %get-tuple-element.31), channel_id=1, source_target_pairs={{0,0},{4,4},{8,8},{12,12},{16,16},{20,20},{24,24},{28,28},{32,32},... | collective-permute-start | bytes 147464 | tf_op jit(solution)/shard_map/ppermute | solution.py:56
  80.9 4.2 %collective-permute-start.9 = (bf16[8,3072]{1,0:T(8,128)(2,1)S(1)}, bf16[8,3072]{1,0:T(8,128)(2,1)S(1)}, u32[]{:S(2)}, u32[]{:S(2)}) collective-permute-start(bf16[8,3072]{1,0:T(8,128)(2,1)S(1)} %get-tuple-element.32), channel_id=1, source_target_pairs={{0,4},{4,8},{8,12},{12,16},{16,20},{20,24},{24,28},{28,32},{32,36}... | collective-permute-start | bytes 147464 | tf_op jit(solution)/shard_map/ppermute | solution.py:56
  86.3 10.6 %copy-start.5 = (bf16[1,8,512]{2,1,0:T(8,128)(2,1)S(1)}, bf16[1,8,512]{2,1,0:T(8,128)(2,1)}, u32[]{:S(2)}) copy-start(bf16[1,8,512]{2,1,0:T(8,128)(2,1)} %param.22) | copy-start | bytes 24580
  87.3 8.8 %all-to-all-start.1 = ((bf16[4,2,12288]{2,1,0:T(2,128)(2,1)}), bf16[4,2,12288]{2,1,0:T(2,128)(2,1)S(1)}, u32[]{:S(2)}, u32[]{:S(2)}) async-start(bf16[4,2,12288]{2,1,0:T(2,128)(2,1)} %reshape.339), calls=%async_computation.1 | async-start | bytes 393216 | tf_op jit(solution)/shard_map/all_to_all | solution.py:203
  97.8 7.5 %all-to-all-start.2 = ((f32[4,8,192]{2,1,0:T(8,128)}), f32[4,8,192]{2,1,0:T(8,128)S(1)}, u32[]{:S(2)}, u32[]{:S(2)}) async-start(f32[4,8,192]{2,1,0:T(8,128)} %broadcast_in_dim.83), calls=%async_computation.2 | async-start | bytes 65536 | tf_op jit(solution)/shard_map/all_to_all | solution.py:46
  117.6 41.3 %copy-start.1 = (f32[1,512,192]{1,2,0:T(8,128)S(1)}, f32[1,512,192]{1,2,0:T(8,128)}, u32[]{:S(2)}) copy-start(f32[1,512,192]{1,2,0:T(8,128)} %param.20) | copy-start | bytes 1179652
  134.0 16.9 %all-to-all-start.5 = ((f32[64,2,192]{2,1,0:T(2,128)}), f32[64,2,192]{2,1,0:T(2,128)}, u32[]{:S(2)}, u32[]{:S(2)}) async-start(f32[64,2,192]{2,1,0:T(2,128)} %broadcast_in_dim.84), calls=%async_computation.5 | async-start | bytes 262144 | tf_op jit(solution)/shard_map/all_to_all | solution.py:46
  160.1 14.7 %copy-start.4 = (f32[1,512,192]{1,2,0:T(8,128)S(1)}, f32[1,512,192]{1,2,0:T(8,128)}, u32[]{:S(2)}) copy-start(f32[1,512,192]{1,2,0:T(8,128)} %param.19) | copy-start | bytes 1179652
  176.5 8.4 %collective-permute-start.15 = (bf16[8,64,48]{2,1,0:T(8,128)(2,1)S(1)}, bf16[8,64,48]{2,1,0:T(8,128)(2,1)S(1)}, u32[]{:S(2)}, u32[]{:S(2)}) collective-permute-start(bf16[8,64,48]{2,1,0:T(8,128)(2,1)S(1)} %get-tuple-element.12), channel_id=1, source_target_pairs={{0,1},{1,2},{2,3},{3,0},{4,5},{5,6},{6,7},{7,4},{8,9},{9,10},{10,1... | collective-permute-start | bytes 147464 | tf_op jit(solution)/shard_map/ppermute | solution.py:30
  178.8 7.3 %collective-permute-start.14 = (bf16[8,64,48]{2,1,0:T(8,128)(2,1)S(1)}, bf16[8,64,48]{2,1,0:T(8,128)(2,1)S(1)}, u32[]{:S(2)}, u32[]{:S(2)}) collective-permute-start(bf16[8,64,48]{2,1,0:T(8,128)(2,1)S(1)} %get-tuple-element.13), channel_id=1, source_target_pairs={{0,2},{1,3},{2,0},{3,1},{4,6},{5,7},{6,4},{7,5},{8,10},{9,11},{10,... | collective-permute-start | bytes 147464 | tf_op jit(solution)/shard_map/ppermute | solution.py:30
  182.4 7.4 %collective-permute-start.13 = (bf16[8,64,48]{2,1,0:T(8,128)(2,1)S(1)}, bf16[8,64,48]{2,1,0:T(8,128)(2,1)S(1)}, u32[]{:S(2)}, u32[]{:S(2)}) collective-permute-start(bf16[8,64,48]{2,1,0:T(8,128)(2,1)S(1)} %get-tuple-element.14), channel_id=1, source_target_pairs={{0,3},{1,0},{2,1},{3,2},{4,7},{5,4},{6,5},{7,6},{8,11},{9,8},{10,9... | collective-permute-start | bytes 147464 | tf_op jit(solution)/shard_map/ppermute | solution.py:30
  190.8 18.1 %copy-start.7 = (bf16[5,8,16]{2,1,0:T(8,128)(2,1)S(1)}, bf16[5,8,16]{2,1,0:T(8,128)(2,1)}, u32[]{:S(2)}) copy-start(bf16[5,8,16]{2,1,0:T(8,128)(2,1)} %copy-done.6) | copy-start | bytes 3844
  192.5 11.6 %collective-permute-start.16 = (bf16[8,3072]{1,0:T(8,128)(2,1)S(1)}, bf16[8,3072]{1,0:T(8,128)(2,1)S(1)}, u32[]{:S(2)}, u32[]{:S(2)}) collective-permute-start(bf16[8,3072]{1,0:T(8,128)(2,1)S(1)} %get-tuple-element.28), channel_id=1, source_target_pairs={{0,504},{4,508},{8,0},{12,4},{16,8},{20,12},{24,16},{28,20},{32,24... | collective-permute-start | bytes 147464 | tf_op jit(solution)/shard_map/ppermute | solution.py:56
  194.7 13.2 %collective-permute-start.20 = (bf16[8,3072]{1,0:T(8,128)(2,1)S(1)}, bf16[8,3072]{1,0:T(8,128)(2,1)S(1)}, u32[]{:S(2)}, u32[]{:S(2)}) collective-permute-start(bf16[8,3072]{1,0:T(8,128)(2,1)S(1)} %get-tuple-element.24), channel_id=1, source_target_pairs={{0,8},{4,12},{8,16},{12,20},{16,24},{20,28},{24,32},{28,36},{32,40... | collective-permute-start | bytes 147464 | tf_op jit(solution)/shard_map/ppermute | solution.py:56
  197.8 10.1 %collective-permute-start.19 = (bf16[8,3072]{1,0:T(8,128)(2,1)S(1)}, bf16[8,3072]{1,0:T(8,128)(2,1)S(1)}, u32[]{:S(2)}, u32[]{:S(2)}) collective-permute-start(bf16[8,3072]{1,0:T(8,128)(2,1)S(1)} %get-tuple-element.25), channel_id=1, source_target_pairs={{0,4},{4,8},{8,12},{12,16},{16,20},{20,24},{24,28},{28,32},{32,36}... | collective-permute-start | bytes 147464 | tf_op jit(solution)/shard_map/ppermute | solution.py:56
  202.1 5.7 %collective-permute-start.18 = (bf16[8,3072]{1,0:T(8,128)(2,1)S(1)}, bf16[8,3072]{1,0:T(8,128)(2,1)S(1)}, u32[]{:S(2)}, u32[]{:S(2)}) collective-permute-start(bf16[8,3072]{1,0:T(8,128)(2,1)S(1)} %get-tuple-element.26), channel_id=1, source_target_pairs={{0,0},{4,4},{8,8},{12,12},{16,16},{20,20},{24,24},{28,28},{32,32},... | collective-permute-start | bytes 147464 | tf_op jit(solution)/shard_map/ppermute | solution.py:56
  202.2 5.7 %collective-permute-start.17 = (bf16[8,3072]{1,0:T(8,128)(2,1)S(1)}, bf16[8,3072]{1,0:T(8,128)(2,1)S(1)}, u32[]{:S(2)}, u32[]{:S(2)}) collective-permute-start(bf16[8,3072]{1,0:T(8,128)(2,1)S(1)} %get-tuple-element.27), channel_id=1, source_target_pairs={{0,508},{4,0},{8,4},{12,8},{16,12},{20,16},{24,20},{28,24},{32,28}... | collective-permute-start | bytes 147464 | tf_op jit(solution)/shard_map/ppermute | solution.py:56
  209.0 19.8 %copy-start.11 = (s32[32]{0:T(128)S(1)}, s32[32]{0:T(128)}, u32[]{:S(2)}) copy-start(s32[32]{0:T(128)} %copy-done.10) | copy-start | bytes 388
  210.7 16.8 %collective-permute-start.21 = (bf16[8,3072]{1,0:T(8,128)(2,1)S(1)}, bf16[8,3072]{1,0:T(8,128)(2,1)S(1)}, u32[]{:S(2)}, u32[]{:S(2)}) collective-permute-start(bf16[8,3072]{1,0:T(8,128)(2,1)S(1)} %get-tuple-element.23), channel_id=1, source_target_pairs={{0,8},{4,12},{8,16},{12,20},{16,24},{20,28},{24,32},{28,36},{32,40... | collective-permute-start | bytes 147464 | tf_op jit(solution)/shard_map/ppermute | solution.py:56
  212.8 16.0 %collective-permute-start.25 = (bf16[8,3072]{1,0:T(8,128)(2,1)S(1)}, bf16[8,3072]{1,0:T(8,128)(2,1)S(1)}, u32[]{:S(2)}, u32[]{:S(2)}) collective-permute-start(bf16[8,3072]{1,0:T(8,128)(2,1)S(1)} %get-tuple-element.19), channel_id=1, source_target_pairs={{0,504},{4,508},{8,0},{12,4},{16,8},{20,12},{24,16},{28,20},{32,24... | collective-permute-start | bytes 147464 | tf_op jit(solution)/shard_map/ppermute | solution.py:56
  222.0 6.8 %collective-permute-start.24 = (bf16[8,3072]{1,0:T(8,128)(2,1)S(1)}, bf16[8,3072]{1,0:T(8,128)(2,1)S(1)}, u32[]{:S(2)}, u32[]{:S(2)}) collective-permute-start(bf16[8,3072]{1,0:T(8,128)(2,1)S(1)} %get-tuple-element.20), channel_id=1, source_target_pairs={{0,508},{4,0},{8,4},{12,8},{16,12},{20,16},{24,20},{28,24},{32,28}... | collective-permute-start | bytes 147464 | tf_op jit(solution)/shard_map/ppermute | solution.py:56
  224.5 4.2 %collective-permute-start.23 = (bf16[8,3072]{1,0:T(8,128)(2,1)S(1)}, bf16[8,3072]{1,0:T(8,128)(2,1)S(1)}, u32[]{:S(2)}, u32[]{:S(2)}) collective-permute-start(bf16[8,3072]{1,0:T(8,128)(2,1)S(1)} %get-tuple-element.21), channel_id=1, source_target_pairs={{0,0},{4,4},{8,8},{12,12},{16,16},{20,20},{24,24},{28,28},{32,32},... | collective-permute-start | bytes 147464 | tf_op jit(solution)/shard_map/ppermute | solution.py:56
  224.5 4.2 %collective-permute-start.22 = (bf16[8,3072]{1,0:T(8,128)(2,1)S(1)}, bf16[8,3072]{1,0:T(8,128)(2,1)S(1)}, u32[]{:S(2)}, u32[]{:S(2)}) collective-permute-start(bf16[8,3072]{1,0:T(8,128)(2,1)S(1)} %get-tuple-element.22), channel_id=1, source_target_pairs={{0,4},{4,8},{8,12},{12,16},{16,20},{20,24},{24,28},{28,32},{32,36}... | collective-permute-start | bytes 147464 | tf_op jit(solution)/shard_map/ppermute | solution.py:56
  258.5 39.7 %copy-start.2 = (f32[512,192]{0,1:T(8,128)S(1)}, f32[512,192]{0,1:T(8,128)}, u32[]{:S(2)}) copy-start(f32[512,192]{0,1:T(8,128)} %get-tuple-element.44) | copy-start | bytes 1179652
  274.9 16.2 %all-to-all-start.12 = ((f32[64,2,192]{2,1,0:T(2,128)}), f32[64,2,192]{2,1,0:T(2,128)S(1)}, u32[]{:S(2)}, u32[]{:S(2)}) async-start(f32[64,2,192]{2,1,0:T(2,128)} %broadcast_in_dim.88), calls=%async_computation.12 | async-start | bytes 262144 | tf_op jit(solution)/shard_map/all_to_all | solution.py:46
  (3 other events, 6.1 us)
